TPU v7x, 32 devices: a whole 2x2x4 slice. The times are simulated.
32 devices in a mesh: wide: 8 (over y, x, core), narrow: 4 (over z).
Axes of the slice: x: 2, y: 2, z: 4, core: 2. Of those that a mesh axis runs over, the one named last changes fastest.
Arguments:
- image: bfloat16 [2, 256, 256, 256], P(None, 'wide', 'narrow'), may hold values from -6 to 6
- deapodization: float32 [3, 256], replicated, may hold values from 0.5 to 2
- offsets: int32 [32, 8], P(('wide', 'narrow')), may hold values from 0 to 256
- cross_weight: bfloat16 [32, 8, 1536, 1024], P(('wide', 'narrow')), may hold values from -0.1875 to 0.1875
- x_weight: bfloat16 [32, 8, 1536, 256], P(('wide', 'narrow')), may hold values from -0.375 to 0.375
Outputs:
- samples: float32 [32, 8, 2, 1536], P(('wide', 'narrow'))
Inputs may be any that keep to these rules, and one draw needn't show every extreme that they name: `offsets`: each entry is the first row, along the first frequency dimension, of a group's window of 256 rows in one slab.
All inputs are finite; a program needn't handle non-finite values.
Results may differ from a plain program's by a relative error of at most 0.007.
Values may be sent and summed in bfloat16 or wider, within the bound.
A program may use at most 128 MiB of HBM per device.

v0:
```python
import math
import jax
import jax.numpy as jnp
from jax import lax
from jax.sharding import PartitionSpec as P

G = 512
KZ = 64
BX = 256
SAMP = 1536


def shifted(block, axis, distance):
    devices = range(lax.axis_size(axis))
    route = [((i - distance) % len(devices), i) for i in devices]
    return lax.ppermute(block, axis, route)


def block_table(out_rows, inputs, grid_size, lowest):
    frequency = jnp.arange(out_rows, dtype=jnp.int32) + lowest
    position = jnp.arange(inputs, dtype=jnp.int32) - inputs // 2
    phases = jnp.mod(frequency[:, None] * position[None, :], grid_size)
    angles = phases.astype(jnp.float32) * (2.0 * math.pi / grid_size)
    factor = 1.0 / math.sqrt(inputs)
    cosine = (jnp.cos(angles) * factor).astype(jnp.bfloat16)
    sine = (jnp.sin(angles) * factor).astype(jnp.bfloat16)
    real_rows = jnp.stack([cosine, sine], axis=1)
    imag_rows = jnp.stack([-sine, cosine], axis=1)
    return jnp.stack([real_rows, imag_rows], axis=0)


def window_samples(window_rows, cross_rows, window_gain):
    partial_value = jnp.einsum(
        "ms,qcs->cmq", cross_rows, window_rows, preferred_element_type=jnp.float32
    )
    return jnp.sum(partial_value * window_gain.astype(jnp.float32)[None], axis=-1)


def per_device(image, deapodization, offsets, cross_weight, x_weight):
    wide_count = lax.axis_size("wide")
    wide_index = lax.axis_index("wide")
    narrow_index = lax.axis_index("narrow")
    block_x = image.shape[1]
    block_y = image.shape[2]
    image_width = image.shape[3]
    scale_x = lax.dynamic_slice_in_dim(deapodization[0], wide_index * block_x, block_x)
    scale_y = lax.dynamic_slice_in_dim(deapodization[1], narrow_index * block_y, block_y)
    weighted = (
        image.astype(jnp.float32)
        * scale_x[None, :, None, None]
        * scale_y[None, None, :, None]
        * deapodization[2][None, None, None, :]
    ).astype(jnp.bfloat16)
    z_table = block_table(KZ, image_width, G, -(KZ // 2))
    band_data = (
        jnp.einsum("okcz,cxyz->xyko", z_table, weighted, preferred_element_type=jnp.float32)
        .astype(jnp.bfloat16)
        .reshape(block_x, block_y, 2 * KZ)
    )
    line_table = block_table(G, image_width, G, -(G // 2))
    pieces = lax.all_to_all(band_data, "narrow", split_axis=2, concat_axis=1, tiled=True)
    item_count = pieces.shape[0]
    band_depth = pieces.shape[2] // 2
    unpacked = pieces.reshape(item_count, image_width, band_depth, 2)
    product = jnp.einsum(
        "oqcy,xykc->xoqk", line_table, unpacked, preferred_element_type=jnp.float32
    )
    columns = product.astype(jnp.bfloat16).reshape(item_count, 2, G * band_depth)
    slab_lines = lax.all_to_all(columns, "wide", split_axis=2, concat_axis=0, tiled=True)

    def transform_rows(table_rows, source):
        product = jnp.einsum(
            "opcx,xcs->pos", table_rows, source, preferred_element_type=jnp.float32
        )
        return product.astype(jnp.bfloat16)

    def slab_samples(slab_data, slab_index):
        start_row = lax.dynamic_index_in_dim(offsets[0], slab_index, 0, False)
        cross_rows = lax.dynamic_index_in_dim(cross_weight[0], slab_index, 0, False)
        window_gain = lax.dynamic_index_in_dim(x_weight[0], slab_index, 0, False)
        part_table = block_table(BX, image_width, G, start_row - G // 2)
        window_rows = transform_rows(part_table, slab_data)
        return window_samples(window_rows, cross_rows, window_gain)

    def record(results, slab_data, slab_index):
        return lax.dynamic_update_index_in_dim(
            results, slab_samples(slab_data, slab_index), slab_index, 0
        )

    results = jnp.zeros((wide_count, 2, SAMP), jnp.float32)

    def one_hop(hop_count, carried):
        current, results = carried
        incoming = shifted(current, "wide", 1)
        results = record(results, current, jnp.mod(wide_index - hop_count, wide_count))
        return (incoming, results)

    current, results = lax.fori_loop(0, wide_count - 1, one_hop, (slab_lines, results))
    results = record(results, current, jnp.mod(wide_index - (wide_count - 1), wide_count))
    return results[None]


def solution(mesh):
    return jax.shard_map(
        per_device,
        mesh=mesh,
        in_specs=(
            P(None, "wide", "narrow", None),
            P(),
            P(("wide", "narrow"), None),
            P(("wide", "narrow"), None, None, None),
            P(("wide", "narrow"), None, None, None),
        ),
        out_specs=P(("wide", "narrow"), None, None, None),
        check_vma=False,
    )
```

profile of v0, /device:TPU:0, one launch (start us, length us, event | category | flops | bytes accessed | tf_op | source)
XLA Modules:
  0.0 221.7 jit_solution(11140627748605231871)
XLA Ops:
  0.0 1.2 fusion.74
  3.5 2.5 %fusion.34 = bf16[32,64,64,2]{2,1,3,0:T(8,128)(2,1)S(1)} fusion(bf16[1,64,2,256]{3,1,2,0:T(8,128)(2,1)S(1)} %get-tuple-element.269, bf16[1,64,2,256]{3,1,2,0:T(8,128)(2,1)S(1)} %get-tuple-element.268, bf16[2,32,64,256]{3,2,1,0:T(8,128)(2,1)} %param.7, f32[256]{0:T(256)S(1)} %bitcast.160, f32[64]{0:T(128)S(1)} %fusion.67, f32[32]{0:T(128)S(1)} %fusion.66), kind=kOutput, calls=%fused_computation.44 | convolution fusion | flops 274202624 | bytes 2753920 | tf_op jit(solution)/shard_map/okcz,cxyz->xyko/dot_general | solution.py:56
  6.1 1.6 copy.31
  7.7 1.5 reshape.794
  9.3 6.3 %all-to-all-start = ((bf16[4,2,32768]{2,1,0:T(2,128)(2,1)}), bf16[4,2,32768]{2,1,0:T(2,128)(2,1)S(1)}, u32[]{:S(2)}, u32[]{:S(2)}) async-start(bf16[4,2,32768]{2,1,0:T(2,128)(2,1)} %reshape.794), calls=%async_computation | async-start | bytes 1048576 | tf_op jit(solution)/shard_map/all_to_all | solution.py:61
  15.6 2.2 fusion.62
  17.8 2.5 %multiply_convert_fusion.3 = (bf16[512,1,256]{2,0,1:T(8,128)(2,1)S(1)}, bf16[512,1,256]{2,0,1:T(8,128)(2,1)S(1)}) fusion(s32[256]{0:T(256)S(1)} %get-tuple-element.280, s32[512]{0:T(512)S(1)} %iota_add_fusion.2), kind=kLoop, calls=%fused_computation.66 | loop fusion | flops 2359296 | bytes 527360 | tf_op jit(solution)/shard_map/convert_element_type | solution.py:26
  20.5 9.6 %all-to-all-done = bf16[4,2,32768]{2,1,0:T(2,128)(2,1)S(1)} async-done(((bf16[4,2,32768]{2,1,0:T(2,128)(2,1)}), bf16[4,2,32768]{2,1,0:T(2,128)(2,1)S(1)}, u32[]{:S(2)}, u32[]{:S(2)}) %all-to-all-start) | async-done | bytes 524320 | tf_op jit(solution)/shard_map/all_to_all | solution.py:61
  31.7 1.5 reshape.778
  33.1 1.8 fusion.37
  35.0 5.1 %copy.35 = bf16[32,2,512,16]{0,3,2,1:T(8,128)(2,1)} copy(bf16[32,2,512,16]{2,3,1,0:T(8,128)(2,1)S(1)} %fusion.37) | data formatting | bytes 2097152 | tf_op jit(solution)/shard_map/convert_element_type | solution.py:68
  40.0 10.1 %copy.69 = bf16[32,2,8192]{0,1,2:T(2,128)(2,1)} copy(bf16[32,2,8192]{0,2,1:T(8,128)(2,1)} %bitcast.154) | data formatting | bytes 2097152 | tf_op jit(solution)/shard_map/reshape | solution.py:68
  50.1 7.8 %reshape.796 = bf16[8,2,32768]{2,1,0:T(2,128)(2,1)} reshape(bf16[8192,2,32]{2,1,0:T(2,128)(2,1)} %bitcast.155) | data formatting | bytes 2097152
  57.9 3.7 %all-to-all-start.1 = ((bf16[8,2,32768]{2,1,0:T(2,128)(2,1)}), bf16[8,2,32768]{2,1,0:T(2,128)(2,1)S(1)}, u32[]{:S(2)}, u32[]{:S(2)}) async-start(bf16[8,2,32768]{2,1,0:T(2,128)(2,1)} %reshape.796), calls=%async_computation.1 | async-start | bytes 2097152 | tf_op jit(solution)/shard_map/all_to_all | solution.py:69
  61.7 1.3 bitcast_convert_fusion.5
  62.9 1.7 copy.42
  65.7 1.3 multiply_convert_fusion.5
  67.0 10.0 %all-to-all-done.1 = bf16[8,2,32768]{2,1,0:T(2,128)(2,1)S(1)} async-done(((bf16[8,2,32768]{2,1,0:T(2,128)(2,1)}), bf16[8,2,32768]{2,1,0:T(2,128)(2,1)S(1)}, u32[]{:S(2)}, u32[]{:S(2)}) %all-to-all-start.1) | async-done | bytes 1048608 | tf_op jit(solution)/shard_map/all_to_all | solution.py:69
  77.0 4.5 %reshape.797 = bf16[8192,2,32]{2,1,0:T(2,128)(2,1)} reshape(bf16[8,2,32768]{2,1,0:T(2,128)(2,1)S(1)} %all-to-all-done.1) | data formatting | bytes 2097152
  81.6 10.4 %copy.57 = bf16[32,2,8,1024]{3,0,2,1:T(8,128)(2,1)} copy(bf16[32,2,8,1024]{0,1,3,2:T(2,128)(2,1)} %bitcast.153) | data formatting | bytes 2097152 | tf_op jit(solution)/shard_map/all_to_all | solution.py:69
  92.0 123.9 %while.18 = (s32[]{:T(128)}, bf16[256,2,1024]{2,0,1:T(8,128)(2,1)}, f32[8,2,1536]{2,1,0:T(2,128)S(1)}, s32[]{:T(128)}, s32[1,8]{1,0:T(1,128)S(1)}, /*index=5*/bf...) while((s32[]{:T(128)}, bf16[256,2,1024]{2,0,1:T(8,128)(2,1)}, ...), condition=%wide.region_2.3_spmd, body=%wide.region_0.2_spmd.sunk | while | flops 2152920576 | bytes 19441996 | solution.py:98
  92.0 2.3 %copy.77 = bf16[256,2,1024]{2,0,1:T(8,128)(2,1)} copy(bf16[256,2,1024]{2,0,1:T(8,128)(2,1)} %get-tuple-element.348) | data formatting | bytes 2097152 | tf_op jit(solution)/shard_map
  95.5 1.3 multiply_convert_fusion.10
  96.8 1.1 fusion.87
  97.9 1.2 constant_dynamic-slice_fusion.6
  99.6 4.6 %fusion.88 = f32[2,1536]{1,0:T(2,128)S(1)} fusion(f32[1536,256]{0,1:T(8,128)S(1)} %bitcast_convert_fusion.7, bf16[1,8,1536,1024]{3,2,1,0:T(8,128)(2,1)} %get-tuple-element.363, s32[]{:T(128)S(6)} %select_n.233, bf16[256,2,1024]{2,0,1:T(8,128)(2,1)} %copy.77, bf16[1,256,2,256]{3,1,2,0:T(8,128)(2,1)S(1)} %get-tuple-element.334, ...), kind=kOutput, calls=%fused_computation.5.clone.1 | convolution fusion | flops 2149839872 | bytes 6303748 | tf_op jit(solution)/shard_map/while/body/eval_jaxpr/ms,qcs->cmq/dot_general | solution.py:33
  104.2 5.5 %collective-permute-done = bf16[256,2,1024]{2,0,1:T(8,128)(2,1)} collective-permute-done((bf16[256,2,1024]{2,0,1:T(8,128)(2,1)}, bf16[256,2,1024]{2,0,1:T(8,128)(2,1)}, u32[]{:S(2)}, u32[]{:S(2)}) %collective-permute-start) | collective-permute-done | bytes 1048608 | tf_op jit(solution)/shard_map/while/body/eval_jaxpr/ppermute | solution.py:16
  109.7 2.3 %copy.77 = bf16[256,2,1024]{2,0,1:T(8,128)(2,1)} copy(bf16[256,2,1024]{2,0,1:T(8,128)(2,1)} %get-tuple-element.348) | data formatting | bytes 2097152 | tf_op jit(solution)/shard_map
  113.2 1.3 multiply_convert_fusion.10
  114.5 1.1 fusion.87
  115.6 1.2 constant_dynamic-slice_fusion.6
  117.3 4.6 %fusion.88 = f32[2,1536]{1,0:T(2,128)S(1)} fusion(f32[1536,256]{0,1:T(8,128)S(1)} %bitcast_convert_fusion.7, bf16[1,8,1536,1024]{3,2,1,0:T(8,128)(2,1)} %get-tuple-element.363, s32[]{:T(128)S(6)} %select_n.233, bf16[256,2,1024]{2,0,1:T(8,128)(2,1)} %copy.77, bf16[1,256,2,256]{3,1,2,0:T(8,128)(2,1)S(1)} %get-tuple-element.334, ...), kind=kOutput, calls=%fused_computation.5.clone.1 | convolution fusion | flops 2149839872 | bytes 6303748 | tf_op jit(solution)/shard_map/while/body/eval_jaxpr/ms,qcs->cmq/dot_general | solution.py:33
  121.9 5.5 %collective-permute-done = bf16[256,2,1024]{2,0,1:T(8,128)(2,1)} collective-permute-done((bf16[256,2,1024]{2,0,1:T(8,128)(2,1)}, bf16[256,2,1024]{2,0,1:T(8,128)(2,1)}, u32[]{:S(2)}, u32[]{:S(2)}) %collective-permute-start) | collective-permute-done | bytes 1048608 | tf_op jit(solution)/shard_map/while/body/eval_jaxpr/ppermute | solution.py:16
  127.4 2.3 %copy.77 = bf16[256,2,1024]{2,0,1:T(8,128)(2,1)} copy(bf16[256,2,1024]{2,0,1:T(8,128)(2,1)} %get-tuple-element.348) | data formatting | bytes 2097152 | tf_op jit(solution)/shard_map
  130.9 1.3 multiply_convert_fusion.10
  132.2 1.1 fusion.87
  133.3 1.2 constant_dynamic-slice_fusion.6
  135.0 4.6 %fusion.88 = f32[2,1536]{1,0:T(2,128)S(1)} fusion(f32[1536,256]{0,1:T(8,128)S(1)} %bitcast_convert_fusion.7, bf16[1,8,1536,1024]{3,2,1,0:T(8,128)(2,1)} %get-tuple-element.363, s32[]{:T(128)S(6)} %select_n.233, bf16[256,2,1024]{2,0,1:T(8,128)(2,1)} %copy.77, bf16[1,256,2,256]{3,1,2,0:T(8,128)(2,1)S(1)} %get-tuple-element.334, ...), kind=kOutput, calls=%fused_computation.5.clone.1 | convolution fusion | flops 2149839872 | bytes 6303748 | tf_op jit(solution)/shard_map/while/body/eval_jaxpr/ms,qcs->cmq/dot_general | solution.py:33
  139.6 5.5 %collective-permute-done = bf16[256,2,1024]{2,0,1:T(8,128)(2,1)} collective-permute-done((bf16[256,2,1024]{2,0,1:T(8,128)(2,1)}, bf16[256,2,1024]{2,0,1:T(8,128)(2,1)}, u32[]{:S(2)}, u32[]{:S(2)}) %collective-permute-start) | collective-permute-done | bytes 1048608 | tf_op jit(solution)/shard_map/while/body/eval_jaxpr/ppermute | solution.py:16
  145.1 2.3 %copy.77 = bf16[256,2,1024]{2,0,1:T(8,128)(2,1)} copy(bf16[256,2,1024]{2,0,1:T(8,128)(2,1)} %get-tuple-element.348) | data formatting | bytes 2097152 | tf_op jit(solution)/shard_map
  148.6 1.3 multiply_convert_fusion.10
  149.9 1.1 fusion.87
  151.0 1.2 constant_dynamic-slice_fusion.6
  152.7 4.6 %fusion.88 = f32[2,1536]{1,0:T(2,128)S(1)} fusion(f32[1536,256]{0,1:T(8,128)S(1)} %bitcast_convert_fusion.7, bf16[1,8,1536,1024]{3,2,1,0:T(8,128)(2,1)} %get-tuple-element.363, s32[]{:T(128)S(6)} %select_n.233, bf16[256,2,1024]{2,0,1:T(8,128)(2,1)} %copy.77, bf16[1,256,2,256]{3,1,2,0:T(8,128)(2,1)S(1)} %get-tuple-element.334, ...), kind=kOutput, calls=%fused_computation.5.clone.1 | convolution fusion | flops 2149839872 | bytes 6303748 | tf_op jit(solution)/shard_map/while/body/eval_jaxpr/ms,qcs->cmq/dot_general | solution.py:33
  157.3 5.5 %collective-permute-done = bf16[256,2,1024]{2,0,1:T(8,128)(2,1)} collective-permute-done((bf16[256,2,1024]{2,0,1:T(8,128)(2,1)}, bf16[256,2,1024]{2,0,1:T(8,128)(2,1)}, u32[]{:S(2)}, u32[]{:S(2)}) %collective-permute-start) | collective-permute-done | bytes 1048608 | tf_op jit(solution)/shard_map/while/body/eval_jaxpr/ppermute | solution.py:16
  162.8 2.3 %copy.77 = bf16[256,2,1024]{2,0,1:T(8,128)(2,1)} copy(bf16[256,2,1024]{2,0,1:T(8,128)(2,1)} %get-tuple-element.348) | data formatting | bytes 2097152 | tf_op jit(solution)/shard_map
  166.4 1.3 multiply_convert_fusion.10
  167.6 1.1 fusion.87
  168.7 1.2 constant_dynamic-slice_fusion.6
  170.4 4.6 %fusion.88 = f32[2,1536]{1,0:T(2,128)S(1)} fusion(f32[1536,256]{0,1:T(8,128)S(1)} %bitcast_convert_fusion.7, bf16[1,8,1536,1024]{3,2,1,0:T(8,128)(2,1)} %get-tuple-element.363, s32[]{:T(128)S(6)} %select_n.233, bf16[256,2,1024]{2,0,1:T(8,128)(2,1)} %copy.77, bf16[1,256,2,256]{3,1,2,0:T(8,128)(2,1)S(1)} %get-tuple-element.334, ...), kind=kOutput, calls=%fused_computation.5.clone.1 | convolution fusion | flops 2149839872 | bytes 6303748 | tf_op jit(solution)/shard_map/while/body/eval_jaxpr/ms,qcs->cmq/dot_general | solution.py:33
  175.0 5.5 %collective-permute-done = bf16[256,2,1024]{2,0,1:T(8,128)(2,1)} collective-permute-done((bf16[256,2,1024]{2,0,1:T(8,128)(2,1)}, bf16[256,2,1024]{2,0,1:T(8,128)(2,1)}, u32[]{:S(2)}, u32[]{:S(2)}) %collective-permute-start) | collective-permute-done | bytes 1048608 | tf_op jit(solution)/shard_map/while/body/eval_jaxpr/ppermute | solution.py:16
  180.5 2.3 %copy.77 = bf16[256,2,1024]{2,0,1:T(8,128)(2,1)} copy(bf16[256,2,1024]{2,0,1:T(8,128)(2,1)} %get-tuple-element.348) | data formatting | bytes 2097152 | tf_op jit(solution)/shard_map
  184.1 1.3 multiply_convert_fusion.10
  185.3 1.1 fusion.87
  186.4 1.2 constant_dynamic-slice_fusion.6
  188.1 4.6 %fusion.88 = f32[2,1536]{1,0:T(2,128)S(1)} fusion(f32[1536,256]{0,1:T(8,128)S(1)} %bitcast_convert_fusion.7, bf16[1,8,1536,1024]{3,2,1,0:T(8,128)(2,1)} %get-tuple-element.363, s32[]{:T(128)S(6)} %select_n.233, bf16[256,2,1024]{2,0,1:T(8,128)(2,1)} %copy.77, bf16[1,256,2,256]{3,1,2,0:T(8,128)(2,1)S(1)} %get-tuple-element.334, ...), kind=kOutput, calls=%fused_computation.5.clone.1 | convolution fusion | flops 2149839872 | bytes 6303748 | tf_op jit(solution)/shard_map/while/body/eval_jaxpr/ms,qcs->cmq/dot_general | solution.py:33
  192.7 5.5 %collective-permute-done = bf16[256,2,1024]{2,0,1:T(8,128)(2,1)} collective-permute-done((bf16[256,2,1024]{2,0,1:T(8,128)(2,1)}, bf16[256,2,1024]{2,0,1:T(8,128)(2,1)}, u32[]{:S(2)}, u32[]{:S(2)}) %collective-permute-start) | collective-permute-done | bytes 1048608 | tf_op jit(solution)/shard_map/while/body/eval_jaxpr/ppermute | solution.py:16
  198.2 2.3 %copy.77 = bf16[256,2,1024]{2,0,1:T(8,128)(2,1)} copy(bf16[256,2,1024]{2,0,1:T(8,128)(2,1)} %get-tuple-element.348) | data formatting | bytes 2097152 | tf_op jit(solution)/shard_map
  201.8 1.3 multiply_convert_fusion.10
  203.0 1.1 fusion.87
  204.1 1.2 constant_dynamic-slice_fusion.6
  205.8 4.6 %fusion.88 = f32[2,1536]{1,0:T(2,128)S(1)} fusion(f32[1536,256]{0,1:T(8,128)S(1)} %bitcast_convert_fusion.7, bf16[1,8,1536,1024]{3,2,1,0:T(8,128)(2,1)} %get-tuple-element.363, s32[]{:T(128)S(6)} %select_n.233, bf16[256,2,1024]{2,0,1:T(8,128)(2,1)} %copy.77, bf16[1,256,2,256]{3,1,2,0:T(8,128)(2,1)S(1)} %get-tuple-element.334, ...), kind=kOutput, calls=%fused_computation.5.clone.1 | convolution fusion | flops 2149839872 | bytes 6303748 | tf_op jit(solution)/shard_map/while/body/eval_jaxpr/ms,qcs->cmq/dot_general | solution.py:33
  210.4 5.5 %collective-permute-done = bf16[256,2,1024]{2,0,1:T(8,128)(2,1)} collective-permute-done((bf16[256,2,1024]{2,0,1:T(8,128)(2,1)}, bf16[256,2,1024]{2,0,1:T(8,128)(2,1)}, u32[]{:S(2)}, u32[]{:S(2)}) %collective-permute-start) | collective-permute-done | bytes 1048608 | tf_op jit(solution)/shard_map/while/body/eval_jaxpr/ppermute | solution.py:16
  215.9 5.1 %fusion.29 = f32[2,1536]{1,0:T(2,128)S(1)} fusion(f32[1536,256]{0,1:T(8,128)} %copy.42, bf16[1,8,1536,1024]{3,2,1,0:T(8,128)(2,1)} %get-tuple-element.371, s32[]{:T(128)S(6)} %select_n.180, bf16[256,2,1024]{2,0,1:T(8,128)(2,1)} %get-tuple-element.215, bf16[1,256,2,256]{3,1,2,0:T(8,128)(2,1)S(1)} %get-tuple-element.267, ...), kind=kOutput, calls=%fused_computation.43 | convolution fusion | flops 2150626304 | bytes 6303748 | tf_op jit(solution)/shard_map/ms,qcs->cmq/dot_general | solution.py:33
  (69 shorter events, 18.0 us)
Async XLA Ops:
  9.3 20.8 %all-to-all-start = ((bf16[4,2,32768]{2,1,0:T(2,128)(2,1)}), bf16[4,2,32768]{2,1,0:T(2,128)(2,1)S(1)}, u32[]{:S(2)}, u32[]{:S(2)}) async-start(bf16[4,2,32768]{2,1,0:T(2,128)(2,1)} %reshape.794), calls=%async_computation | async-start | bytes 1048576 | tf_op jit(solution)/shard_map/all_to_all | solution.py:61
  57.9 19.1 %all-to-all-start.1 = ((bf16[8,2,32768]{2,1,0:T(2,128)(2,1)}), bf16[8,2,32768]{2,1,0:T(2,128)(2,1)S(1)}, u32[]{:S(2)}, u32[]{:S(2)}) async-start(bf16[8,2,32768]{2,1,0:T(2,128)(2,1)} %reshape.796), calls=%async_computation.1 | async-start | bytes 2097152 | tf_op jit(solution)/shard_map/all_to_all | solution.py:69
  81.5 10.4 %copy-start.1 = (s32[1,8]{1,0:T(1,128)S(1)}, s32[1,8]{1,0:T(1,128)}, u32[]{:S(2)}) copy-start(s32[1,8]{1,0:T(1,128)} %param.9) | copy-start | bytes 100
  94.3 15.4 %collective-permute-start = (bf16[256,2,1024]{2,0,1:T(8,128)(2,1)}, bf16[256,2,1024]{2,0,1:T(8,128)(2,1)}, u32[]{:S(2)}, u32[]{:S(2)}) collective-permute-start(bf16[256,2,1024]{2,0,1:T(8,128)(2,1)} %copy.77), channel_id=1, source_target_pairs={{28,0},{0,4},{4,8},{8,12},{12,16},{16,20},{20,24},{24,28},{29,1},{... | collective-permute-start | bytes 3145736 | tf_op jit(solution)/shard_map/while/body/eval_jaxpr/ppermute | solution.py:16
  112.0 15.4 %collective-permute-start = (bf16[256,2,1024]{2,0,1:T(8,128)(2,1)}, bf16[256,2,1024]{2,0,1:T(8,128)(2,1)}, u32[]{:S(2)}, u32[]{:S(2)}) collective-permute-start(bf16[256,2,1024]{2,0,1:T(8,128)(2,1)} %copy.77), channel_id=1, source_target_pairs={{28,0},{0,4},{4,8},{8,12},{12,16},{16,20},{20,24},{24,28},{29,1},{... | collective-permute-start | bytes 3145736 | tf_op jit(solution)/shard_map/while/body/eval_jaxpr/ppermute | solution.py:16
  129.7 15.4 %collective-permute-start = (bf16[256,2,1024]{2,0,1:T(8,128)(2,1)}, bf16[256,2,1024]{2,0,1:T(8,128)(2,1)}, u32[]{:S(2)}, u32[]{:S(2)}) collective-permute-start(bf16[256,2,1024]{2,0,1:T(8,128)(2,1)} %copy.77), channel_id=1, source_target_pairs={{28,0},{0,4},{4,8},{8,12},{12,16},{16,20},{20,24},{24,28},{29,1},{... | collective-permute-start | bytes 3145736 | tf_op jit(solution)/shard_map/while/body/eval_jaxpr/ppermute | solution.py:16
  147.4 15.4 %collective-permute-start = (bf16[256,2,1024]{2,0,1:T(8,128)(2,1)}, bf16[256,2,1024]{2,0,1:T(8,128)(2,1)}, u32[]{:S(2)}, u32[]{:S(2)}) collective-permute-start(bf16[256,2,1024]{2,0,1:T(8,128)(2,1)} %copy.77), channel_id=1, source_target_pairs={{28,0},{0,4},{4,8},{8,12},{12,16},{16,20},{20,24},{24,28},{29,1},{... | collective-permute-start | bytes 3145736 | tf_op jit(solution)/shard_map/while/body/eval_jaxpr/ppermute | solution.py:16
  165.1 15.4 %collective-permute-start = (bf16[256,2,1024]{2,0,1:T(8,128)(2,1)}, bf16[256,2,1024]{2,0,1:T(8,128)(2,1)}, u32[]{:S(2)}, u32[]{:S(2)}) collective-permute-start(bf16[256,2,1024]{2,0,1:T(8,128)(2,1)} %copy.77), channel_id=1, source_target_pairs={{28,0},{0,4},{4,8},{8,12},{12,16},{16,20},{20,24},{24,28},{29,1},{... | collective-permute-start | bytes 3145736 | tf_op jit(solution)/shard_map/while/body/eval_jaxpr/ppermute | solution.py:16
  182.8 15.4 %collective-permute-start = (bf16[256,2,1024]{2,0,1:T(8,128)(2,1)}, bf16[256,2,1024]{2,0,1:T(8,128)(2,1)}, u32[]{:S(2)}, u32[]{:S(2)}) collective-permute-start(bf16[256,2,1024]{2,0,1:T(8,128)(2,1)} %copy.77), channel_id=1, source_target_pairs={{28,0},{0,4},{4,8},{8,12},{12,16},{16,20},{20,24},{24,28},{29,1},{... | collective-permute-start | bytes 3145736 | tf_op jit(solution)/shard_map/while/body/eval_jaxpr/ppermute | solution.py:16
  200.5 15.4 %collective-permute-start = (bf16[256,2,1024]{2,0,1:T(8,128)(2,1)}, bf16[256,2,1024]{2,0,1:T(8,128)(2,1)}, u32[]{:S(2)}, u32[]{:S(2)}) collective-permute-start(bf16[256,2,1024]{2,0,1:T(8,128)(2,1)} %copy.77), channel_id=1, source_target_pairs={{28,0},{0,4},{4,8},{8,12},{12,16},{16,20},{20,24},{24,28},{29,1},{... | collective-permute-start | bytes 3145736 | tf_op jit(solution)/shard_map/while/body/eval_jaxpr/ppermute | solution.py:16
  215.9 5.1 %copy-start = (f32[8,2,1536]{2,1,0:T(2,128)}, f32[8,2,1536]{2,1,0:T(2,128)S(1)}, u32[]{:S(2)}) copy-start(f32[8,2,1536]{2,1,0:T(2,128)S(1)} %get-tuple-element.214) | copy-start | bytes 294916
where the time goes:
time: 223 us; the launch traced here: 222 us
  local copies, waits for them, and re-layouts  73.5 us (33%)
  waiting for transfers between devices  58.2 us (26%)
  matrix products  41.5 us (19%)
  other arithmetic  37.8 us (17%)
  starting transfers between devices  10.1 us (5%)
    ppermute x7, waiting for transfers between devices, shifted(): return lax.ppermute(block, axis, route)  38.5 us
    dot_general x8, matrix products, window_samples(): jnp.einsum('ms,qcs->cmq', cross_rows, window_rows, preferred_element_type...  37.1 us
    another operation x7, local copies, waits for them, and re-layouts  15.8 us
    unnamed x8, local copies, waits for them, and re-layouts  14.6 us
    convert_element_type x10, other arithmetic, block_table(): sine = (jnp.sin(angles) * factor).astype(jnp.bfloat16)  13.1 us
    neg x10, other arithmetic, block_table(): imag_rows = jnp.stack([-sine, cosine], axis=1)  11.1 us
    all_to_all x1, local copies, waits for them, and re-layouts, per_device(): lax.all_to_all(columns, 'wide', split_axis=2, concat_axis=0, tiled=True)  10.4 us
    dynamic_slice x14, local copies, waits for them, and re-layouts, slab_samples(): window_gain = lax.dynamic_index_in_dim(x_weight[0], slab_index, 0, False)  10.3 us
  transfers between devices with their start and end apart: 9, of which 9 were waited for; matrix products, arithmetic and copies ran while one was open for 36% of the time, Pallas kernels for 0%

commit v1 on v0

--- a/solution.py
+++ b/solution.py
@@ -66,7 +66,10 @@
         "oqcy,xykc->xoqk", line_table, unpacked, preferred_element_type=jnp.float32
     )
     columns = product.astype(jnp.bfloat16).reshape(item_count, 2, G * band_depth)
-    slab_lines = lax.all_to_all(columns, "wide", split_axis=2, concat_axis=0, tiled=True)
+    slab_lines = jnp.concatenate(
+        lax.all_to_all(jnp.stack(jnp.split(columns, lax.axis_size("wide"), axis=2)), "wide", 0, 0),
+        axis=0,
+    )
 
     def transform_rows(table_rows, source):
         product = jnp.einsum(

time: 223 us -> 204 us (0.915)
  local copies, waits for them, and re-layouts: 73.5 us -> 54.1 us
    reshape x1 -> x0, local copies, waits for them, and re-layouts: 10.1 us -> none  [per_device(): product.astype(jnp.bfloat16).reshape(item_count, 2, G * band_depth)]
    all_to_all x1, local copies, waits for them, and re-layouts: 10.4 us -> 1.07 us  [per_device(): lax.all_to_all(jnp.stack(jnp.split(columns, lax.axis_size('wide'), axis=2...]
    another operation x7 -> x17, local copies, waits for them, and re-layouts: 15.8 us -> 23.5 us
    unnamed x8 -> x13, local copies, waits for them, and re-layouts: 14.6 us -> 6.92 us
  transfers between devices with their start and end apart: 9 -> 9, of which waited for: 9 -> 9; matrix products, arithmetic and copies ran while one was open for 36% -> 39% of each run, Pallas kernels for 0% -> 0%
where the time goes in v1:
time: 204 us; the launch traced here: 202 us
  waiting for transfers between devices  57.7 us (28%)
  local copies, waits for them, and re-layouts  54.1 us (27%)
  matrix products  41.5 us (20%)
  other arithmetic  38.3 us (19%)
  starting transfers between devices  10.1 us (5%)
    ppermute x7, waiting for transfers between devices, shifted(): return lax.ppermute(block, axis, route)  38 us
    dot_general x8, matrix products, window_samples(): jnp.einsum('ms,qcs->cmq', cross_rows, window_rows, preferred_element_type...  37.1 us
    another operation x7, local copies, waits for them, and re-layouts  15.9 us
    convert_element_type x10, other arithmetic, block_table(): sine = (jnp.sin(angles) * factor).astype(jnp.bfloat16)  13.1 us
    neg x10, other arithmetic, block_table(): imag_rows = jnp.stack([-sine, cosine], axis=1)  11.1 us
    dynamic_slice x14, local copies, waits for them, and re-layouts, slab_samples(): window_gain = lax.dynamic_index_in_dim(x_weight[0], slab_index, 0, False)  10.3 us
    all_to_all x1, waiting for transfers between devices, per_device(): lax.all_to_all(jnp.stack(jnp.split(columns, lax.axis_size('wide'), axis=2...  10 us
    all_to_all x1, waiting for transfers between devices, per_device(): lax.all_to_all(band_data, 'narrow', split_axis=2, concat_axis=1, tiled=True)  9.64 us
  transfers between devices with their start and end apart: 9, of which 9 were waited for; matrix products, arithmetic and copies ran while one was open for 39% of the time, Pallas kernels for 0%

profile of v1, /device:TPU:0, one launch (start us, length us, event | category | flops | bytes accessed | tf_op | source)
XLA Modules:
  0.0 202.3 jit_solution(1386031301162541681)
XLA Ops:
  0.0 1.2 fusion.74
  3.5 2.5 %fusion.34 = bf16[32,64,64,2]{2,1,3,0:T(8,128)(2,1)S(1)} fusion(bf16[1,64,2,256]{3,1,2,0:T(8,128)(2,1)S(1)} %get-tuple-element.277, bf16[1,64,2,256]{3,1,2,0:T(8,128)(2,1)S(1)} %get-tuple-element.276, bf16[2,32,64,256]{3,2,1,0:T(8,128)(2,1)} %param.7, f32[256]{0:T(256)S(1)} %bitcast.166, f32[64]{0:T(128)S(1)} %fusion.67, f32[32]{0:T(128)S(1)} %fusion.66), kind=kOutput, calls=%fused_computation.44 | convolution fusion | flops 274202624 | bytes 2753920 | tf_op jit(solution)/shard_map/okcz,cxyz->xyko/dot_general | solution.py:56
  6.1 1.6 copy.29
  7.7 1.6 reshape.798
  9.3 6.3 %all-to-all-start = ((bf16[4,2,32768]{2,1,0:T(2,128)(2,1)}), bf16[4,2,32768]{2,1,0:T(2,128)(2,1)S(1)}, u32[]{:S(2)}, u32[]{:S(2)}) async-start(bf16[4,2,32768]{2,1,0:T(2,128)(2,1)} %reshape.798), calls=%async_computation | async-start | bytes 1048576 | tf_op jit(solution)/shard_map/all_to_all | solution.py:61
  15.6 2.2 %fusion.62 = bf16[512,1,256]{2,0,1:T(8,128)(2,1)S(1)} fusion(s32[256]{0:T(256)S(1)} %get-tuple-element.288, s32[512]{0:T(512)S(1)} %iota_add_fusion.2), kind=kLoop, calls=%fused_computation.103 | loop fusion | flops 2490368 | bytes 265216 | tf_op jit(solution)/shard_map/neg | solution.py:28
  17.8 2.5 %multiply_convert_fusion.3 = (bf16[512,1,256]{2,0,1:T(8,128)(2,1)S(1)}, bf16[512,1,256]{2,0,1:T(8,128)(2,1)S(1)}) fusion(s32[256]{0:T(256)S(1)} %get-tuple-element.288, s32[512]{0:T(512)S(1)} %iota_add_fusion.2), kind=kLoop, calls=%fused_computation.74 | loop fusion | flops 2359296 | bytes 527360 | tf_op jit(solution)/shard_map/convert_element_type | solution.py:26
  20.5 9.6 %all-to-all-done = bf16[4,2,32768]{2,1,0:T(2,128)(2,1)S(1)} async-done(((bf16[4,2,32768]{2,1,0:T(2,128)(2,1)}), bf16[4,2,32768]{2,1,0:T(2,128)(2,1)S(1)}, u32[]{:S(2)}, u32[]{:S(2)}) %all-to-all-start) | async-done | bytes 524320 | tf_op jit(solution)/shard_map/all_to_all | solution.py:61
  31.7 1.5 reshape.781
  33.1 1.8 fusion.37
  35.0 5.1 %copy.33 = bf16[32,2,512,16]{0,3,2,1:T(8,128)(2,1)} copy(bf16[32,2,512,16]{2,3,1,0:T(8,128)(2,1)S(1)} %fusion.37) | data formatting | bytes 2097152 | tf_op jit(solution)/shard_map/convert_element_type | solution.py:68
  40.0 3.4 %slice_bitcast_fusion = (bf16[1,32,2,1024]{1,3,2,0:T(8,128)(2,1)S(1)}, bf16[1,32,2,1024]{1,3,2,0:T(8,128)(2,1)S(1)}, bf16[1,32,2,1024]{1,3,2,0:T(8,128)(2,1)S(1)...) fusion(bf16[32,2,8192]{0,2,1:T(8,128)(2,1)} %bitcast.161), kind=kLoop, calls=%fused_computation.60 | loop fusion | bytes 2097152 | tf_op jit(solution)/shard_map/stack | solution.py:70
  43.4 1.2 copy.34
  45.3 1.2 copy.35
  52.4 3.7 %all-to-all-start.1 = ((bf16[8,32,2,1024]{3,1,2,0:T(8,128)(2,1)}), bf16[8,32,2,1024]{3,1,2,0:T(8,128)(2,1)S(1)}, u32[]{:S(2)}, u32[]{:S(2)}) async-start(bf16[8,32,2,1024]{3,1,2,0:T(8,128)(2,1)} %constant_dynamic-update-slice_fusion), calls=%async_computation.1 | async-start | bytes 2097152 | tf_op jit(solution)/shard_map/all_to_all | solution.py:70
  56.1 1.3 bitcast_convert_fusion.5
  57.4 1.6 copy.46
  60.1 1.3 multiply_convert_fusion.5
  61.4 10.0 %all-to-all-done.1 = bf16[8,32,2,1024]{3,1,2,0:T(8,128)(2,1)S(1)} async-done(((bf16[8,32,2,1024]{3,1,2,0:T(8,128)(2,1)}), bf16[8,32,2,1024]{3,1,2,0:T(8,128)(2,1)S(1)}, u32[]{:S(2)}, u32[]{:S(2)}) %all-to-all-start.1) | async-done | bytes 1048608 | tf_op jit(solution)/shard_map/all_to_all | solution.py:70
  71.5 1.1 copy.42
  72.6 124.0 %while.18 = (s32[]{:T(128)}, bf16[256,2,1024]{2,0,1:T(8,128)(2,1)}, f32[8,2,1536]{2,1,0:T(2,128)S(1)}, s32[]{:T(128)}, s32[1,8]{1,0:T(1,128)S(1)}, /*index=5*/bf...) while((s32[]{:T(128)}, bf16[256,2,1024]{2,0,1:T(8,128)(2,1)}, ...), condition=%wide.region_2.3_spmd, body=%wide.region_0.2_spmd.sunk | while | flops 2152920576 | bytes 19441996 | solution.py:101
  72.6 2.3 %copy.84 = bf16[256,2,1024]{2,0,1:T(8,128)(2,1)} copy(bf16[256,2,1024]{2,0,1:T(8,128)(2,1)} %get-tuple-element.356) | data formatting | bytes 2097152 | tf_op jit(solution)/shard_map
  76.2 1.3 multiply_convert_fusion.10
  77.5 1.1 fusion.87
  78.5 1.2 constant_dynamic-slice_fusion.6
  80.3 4.6 %fusion.88 = f32[2,1536]{1,0:T(2,128)S(1)} fusion(f32[1536,256]{0,1:T(8,128)S(1)} %bitcast_convert_fusion.7, bf16[1,8,1536,1024]{3,2,1,0:T(8,128)(2,1)} %get-tuple-element.371, s32[]{:T(128)S(6)} %select_n.233, bf16[256,2,1024]{2,0,1:T(8,128)(2,1)} %copy.84, bf16[1,256,2,256]{3,1,2,0:T(8,128)(2,1)S(1)} %get-tuple-element.342, ...), kind=kOutput, calls=%fused_computation.5.clone.1 | convolution fusion | flops 2149839872 | bytes 6303748 | tf_op jit(solution)/shard_map/while/body/eval_jaxpr/ms,qcs->cmq/dot_general | solution.py:33
  84.9 5.4 %collective-permute-done = bf16[256,2,1024]{2,0,1:T(8,128)(2,1)} collective-permute-done((bf16[256,2,1024]{2,0,1:T(8,128)(2,1)}, bf16[256,2,1024]{2,0,1:T(8,128)(2,1)}, u32[]{:S(2)}, u32[]{:S(2)}) %collective-permute-start) | collective-permute-done | bytes 1048608 | tf_op jit(solution)/shard_map/while/body/eval_jaxpr/ppermute | solution.py:16
  90.3 2.3 %copy.84 = bf16[256,2,1024]{2,0,1:T(8,128)(2,1)} copy(bf16[256,2,1024]{2,0,1:T(8,128)(2,1)} %get-tuple-element.356) | data formatting | bytes 2097152 | tf_op jit(solution)/shard_map
  93.9 1.3 multiply_convert_fusion.10
  95.2 1.1 fusion.87
  96.3 1.2 constant_dynamic-slice_fusion.6
  98.0 4.6 %fusion.88 = f32[2,1536]{1,0:T(2,128)S(1)} fusion(f32[1536,256]{0,1:T(8,128)S(1)} %bitcast_convert_fusion.7, bf16[1,8,1536,1024]{3,2,1,0:T(8,128)(2,1)} %get-tuple-element.371, s32[]{:T(128)S(6)} %select_n.233, bf16[256,2,1024]{2,0,1:T(8,128)(2,1)} %copy.84, bf16[1,256,2,256]{3,1,2,0:T(8,128)(2,1)S(1)} %get-tuple-element.342, ...), kind=kOutput, calls=%fused_computation.5.clone.1 | convolution fusion | flops 2149839872 | bytes 6303748 | tf_op jit(solution)/shard_map/while/body/eval_jaxpr/ms,qcs->cmq/dot_general | solution.py:33
  102.6 5.4 %collective-permute-done = bf16[256,2,1024]{2,0,1:T(8,128)(2,1)} collective-permute-done((bf16[256,2,1024]{2,0,1:T(8,128)(2,1)}, bf16[256,2,1024]{2,0,1:T(8,128)(2,1)}, u32[]{:S(2)}, u32[]{:S(2)}) %collective-permute-start) | collective-permute-done | bytes 1048608 | tf_op jit(solution)/shard_map/while/body/eval_jaxpr/ppermute | solution.py:16
  108.0 2.3 %copy.84 = bf16[256,2,1024]{2,0,1:T(8,128)(2,1)} copy(bf16[256,2,1024]{2,0,1:T(8,128)(2,1)} %get-tuple-element.356) | data formatting | bytes 2097152 | tf_op jit(solution)/shard_map
  111.6 1.3 multiply_convert_fusion.10
  112.9 1.1 fusion.87
  114.0 1.2 constant_dynamic-slice_fusion.6
  115.7 4.6 %fusion.88 = f32[2,1536]{1,0:T(2,128)S(1)} fusion(f32[1536,256]{0,1:T(8,128)S(1)} %bitcast_convert_fusion.7, bf16[1,8,1536,1024]{3,2,1,0:T(8,128)(2,1)} %get-tuple-element.371, s32[]{:T(128)S(6)} %select_n.233, bf16[256,2,1024]{2,0,1:T(8,128)(2,1)} %copy.84, bf16[1,256,2,256]{3,1,2,0:T(8,128)(2,1)S(1)} %get-tuple-element.342, ...), kind=kOutput, calls=%fused_computation.5.clone.1 | convolution fusion | flops 2149839872 | bytes 6303748 | tf_op jit(solution)/shard_map/while/body/eval_jaxpr/ms,qcs->cmq/dot_general | solution.py:33
  120.3 5.4 %collective-permute-done = bf16[256,2,1024]{2,0,1:T(8,128)(2,1)} collective-permute-done((bf16[256,2,1024]{2,0,1:T(8,128)(2,1)}, bf16[256,2,1024]{2,0,1:T(8,128)(2,1)}, u32[]{:S(2)}, u32[]{:S(2)}) %collective-permute-start) | collective-permute-done | bytes 1048608 | tf_op jit(solution)/shard_map/while/body/eval_jaxpr/ppermute | solution.py:16
  125.7 2.3 %copy.84 = bf16[256,2,1024]{2,0,1:T(8,128)(2,1)} copy(bf16[256,2,1024]{2,0,1:T(8,128)(2,1)} %get-tuple-element.356) | data formatting | bytes 2097152 | tf_op jit(solution)/shard_map
  129.3 1.3 multiply_convert_fusion.10
  130.6 1.1 fusion.87
  131.7 1.2 constant_dynamic-slice_fusion.6
  133.4 4.6 %fusion.88 = f32[2,1536]{1,0:T(2,128)S(1)} fusion(f32[1536,256]{0,1:T(8,128)S(1)} %bitcast_convert_fusion.7, bf16[1,8,1536,1024]{3,2,1,0:T(8,128)(2,1)} %get-tuple-element.371, s32[]{:T(128)S(6)} %select_n.233, bf16[256,2,1024]{2,0,1:T(8,128)(2,1)} %copy.84, bf16[1,256,2,256]{3,1,2,0:T(8,128)(2,1)S(1)} %get-tuple-element.342, ...), kind=kOutput, calls=%fused_computation.5.clone.1 | convolution fusion | flops 2149839872 | bytes 6303748 | tf_op jit(solution)/shard_map/while/body/eval_jaxpr/ms,qcs->cmq/dot_general | solution.py:33
  138.0 5.4 %collective-permute-done = bf16[256,2,1024]{2,0,1:T(8,128)(2,1)} collective-permute-done((bf16[256,2,1024]{2,0,1:T(8,128)(2,1)}, bf16[256,2,1024]{2,0,1:T(8,128)(2,1)}, u32[]{:S(2)}, u32[]{:S(2)}) %collective-permute-start) | collective-permute-done | bytes 1048608 | tf_op jit(solution)/shard_map/while/body/eval_jaxpr/ppermute | solution.py:16
  143.4 2.3 %copy.84 = bf16[256,2,1024]{2,0,1:T(8,128)(2,1)} copy(bf16[256,2,1024]{2,0,1:T(8,128)(2,1)} %get-tuple-element.356) | data formatting | bytes 2097152 | tf_op jit(solution)/shard_map
  147.0 1.3 multiply_convert_fusion.10
  148.3 1.1 fusion.87
  149.4 1.2 constant_dynamic-slice_fusion.6
  151.1 4.6 %fusion.88 = f32[2,1536]{1,0:T(2,128)S(1)} fusion(f32[1536,256]{0,1:T(8,128)S(1)} %bitcast_convert_fusion.7, bf16[1,8,1536,1024]{3,2,1,0:T(8,128)(2,1)} %get-tuple-element.371, s32[]{:T(128)S(6)} %select_n.233, bf16[256,2,1024]{2,0,1:T(8,128)(2,1)} %copy.84, bf16[1,256,2,256]{3,1,2,0:T(8,128)(2,1)S(1)} %get-tuple-element.342, ...), kind=kOutput, calls=%fused_computation.5.clone.1 | convolution fusion | flops 2149839872 | bytes 6303748 | tf_op jit(solution)/shard_map/while/body/eval_jaxpr/ms,qcs->cmq/dot_general | solution.py:33
  155.7 5.4 %collective-permute-done = bf16[256,2,1024]{2,0,1:T(8,128)(2,1)} collective-permute-done((bf16[256,2,1024]{2,0,1:T(8,128)(2,1)}, bf16[256,2,1024]{2,0,1:T(8,128)(2,1)}, u32[]{:S(2)}, u32[]{:S(2)}) %collective-permute-start) | collective-permute-done | bytes 1048608 | tf_op jit(solution)/shard_map/while/body/eval_jaxpr/ppermute | solution.py:16
  161.1 2.3 %copy.84 = bf16[256,2,1024]{2,0,1:T(8,128)(2,1)} copy(bf16[256,2,1024]{2,0,1:T(8,128)(2,1)} %get-tuple-element.356) | data formatting | bytes 2097152 | tf_op jit(solution)/shard_map
  164.7 1.3 multiply_convert_fusion.10
  166.0 1.1 fusion.87
  167.1 1.2 constant_dynamic-slice_fusion.6
  168.8 4.6 %fusion.88 = f32[2,1536]{1,0:T(2,128)S(1)} fusion(f32[1536,256]{0,1:T(8,128)S(1)} %bitcast_convert_fusion.7, bf16[1,8,1536,1024]{3,2,1,0:T(8,128)(2,1)} %get-tuple-element.371, s32[]{:T(128)S(6)} %select_n.233, bf16[256,2,1024]{2,0,1:T(8,128)(2,1)} %copy.84, bf16[1,256,2,256]{3,1,2,0:T(8,128)(2,1)S(1)} %get-tuple-element.342, ...), kind=kOutput, calls=%fused_computation.5.clone.1 | convolution fusion | flops 2149839872 | bytes 6303748 | tf_op jit(solution)/shard_map/while/body/eval_jaxpr/ms,qcs->cmq/dot_general | solution.py:33
  173.4 5.4 %collective-permute-done = bf16[256,2,1024]{2,0,1:T(8,128)(2,1)} collective-permute-done((bf16[256,2,1024]{2,0,1:T(8,128)(2,1)}, bf16[256,2,1024]{2,0,1:T(8,128)(2,1)}, u32[]{:S(2)}, u32[]{:S(2)}) %collective-permute-start) | collective-permute-done | bytes 1048608 | tf_op jit(solution)/shard_map/while/body/eval_jaxpr/ppermute | solution.py:16
  178.8 2.3 %copy.84 = bf16[256,2,1024]{2,0,1:T(8,128)(2,1)} copy(bf16[256,2,1024]{2,0,1:T(8,128)(2,1)} %get-tuple-element.356) | data formatting | bytes 2097152 | tf_op jit(solution)/shard_map
  182.4 1.3 multiply_convert_fusion.10
  183.7 1.1 fusion.87
  184.8 1.2 constant_dynamic-slice_fusion.6
  186.5 4.6 %fusion.88 = f32[2,1536]{1,0:T(2,128)S(1)} fusion(f32[1536,256]{0,1:T(8,128)S(1)} %bitcast_convert_fusion.7, bf16[1,8,1536,1024]{3,2,1,0:T(8,128)(2,1)} %get-tuple-element.371, s32[]{:T(128)S(6)} %select_n.233, bf16[256,2,1024]{2,0,1:T(8,128)(2,1)} %copy.84, bf16[1,256,2,256]{3,1,2,0:T(8,128)(2,1)S(1)} %get-tuple-element.342, ...), kind=kOutput, calls=%fused_computation.5.clone.1 | convolution fusion | flops 2149839872 | bytes 6303748 | tf_op jit(solution)/shard_map/while/body/eval_jaxpr/ms,qcs->cmq/dot_general | solution.py:33
  191.1 5.4 %collective-permute-done = bf16[256,2,1024]{2,0,1:T(8,128)(2,1)} collective-permute-done((bf16[256,2,1024]{2,0,1:T(8,128)(2,1)}, bf16[256,2,1024]{2,0,1:T(8,128)(2,1)}, u32[]{:S(2)}, u32[]{:S(2)}) %collective-permute-start) | collective-permute-done | bytes 1048608 | tf_op jit(solution)/shard_map/while/body/eval_jaxpr/ppermute | solution.py:16
  196.5 5.1 %fusion.29 = f32[2,1536]{1,0:T(2,128)S(1)} fusion(f32[1536,256]{0,1:T(8,128)} %copy.46, bf16[1,8,1536,1024]{3,2,1,0:T(8,128)(2,1)} %get-tuple-element.381, s32[]{:T(128)S(6)} %select_n.180, bf16[256,2,1024]{2,0,1:T(8,128)(2,1)} %get-tuple-element.215, bf16[1,256,2,256]{3,1,2,0:T(8,128)(2,1)S(1)} %get-tuple-element.275, ...), kind=kOutput, calls=%fused_computation.43 | convolution fusion | flops 2150626304 | bytes 6303748 | tf_op jit(solution)/shard_map/ms,qcs->cmq/dot_general | solution.py:33
  (83 shorter events, 24.9 us)
Async XLA Ops:
  9.3 20.8 %all-to-all-start = ((bf16[4,2,32768]{2,1,0:T(2,128)(2,1)}), bf16[4,2,32768]{2,1,0:T(2,128)(2,1)S(1)}, u32[]{:S(2)}, u32[]{:S(2)}) async-start(bf16[4,2,32768]{2,1,0:T(2,128)(2,1)} %reshape.798), calls=%async_computation | async-start | bytes 1048576 | tf_op jit(solution)/shard_map/all_to_all | solution.py:61
  52.4 19.1 %all-to-all-start.1 = ((bf16[8,32,2,1024]{3,1,2,0:T(8,128)(2,1)}), bf16[8,32,2,1024]{3,1,2,0:T(8,128)(2,1)S(1)}, u32[]{:S(2)}, u32[]{:S(2)}) async-start(bf16[8,32,2,1024]{3,1,2,0:T(8,128)(2,1)} %constant_dynamic-update-slice_fusion), calls=%async_computation.1 | async-start | bytes 2097152 | tf_op jit(solution)/shard_map/all_to_all | solution.py:70
  57.4 15.2 %copy-start.1 = (s32[1,8]{1,0:T(1,128)S(1)}, s32[1,8]{1,0:T(1,128)}, u32[]{:S(2)}) copy-start(s32[1,8]{1,0:T(1,128)} %param.9) | copy-start | bytes 100
  74.8 15.4 %collective-permute-start = (bf16[256,2,1024]{2,0,1:T(8,128)(2,1)}, bf16[256,2,1024]{2,0,1:T(8,128)(2,1)}, u32[]{:S(2)}, u32[]{:S(2)}) collective-permute-start(bf16[256,2,1024]{2,0,1:T(8,128)(2,1)} %copy.84), channel_id=1, source_target_pairs={{28,0},{0,4},{4,8},{8,12},{12,16},{16,20},{20,24},{24,28},{29,1},{... | collective-permute-start | bytes 3145736 | tf_op jit(solution)/shard_map/while/body/eval_jaxpr/ppermute | solution.py:16
  92.6 15.4 %collective-permute-start = (bf16[256,2,1024]{2,0,1:T(8,128)(2,1)}, bf16[256,2,1024]{2,0,1:T(8,128)(2,1)}, u32[]{:S(2)}, u32[]{:S(2)}) collective-permute-start(bf16[256,2,1024]{2,0,1:T(8,128)(2,1)} %copy.84), channel_id=1, source_target_pairs={{28,0},{0,4},{4,8},{8,12},{12,16},{16,20},{20,24},{24,28},{29,1},{... | collective-permute-start | bytes 3145736 | tf_op jit(solution)/shard_map/while/body/eval_jaxpr/ppermute | solution.py:16
  110.3 15.4 %collective-permute-start = (bf16[256,2,1024]{2,0,1:T(8,128)(2,1)}, bf16[256,2,1024]{2,0,1:T(8,128)(2,1)}, u32[]{:S(2)}, u32[]{:S(2)}) collective-permute-start(bf16[256,2,1024]{2,0,1:T(8,128)(2,1)} %copy.84), channel_id=1, source_target_pairs={{28,0},{0,4},{4,8},{8,12},{12,16},{16,20},{20,24},{24,28},{29,1},{... | collective-permute-start | bytes 3145736 | tf_op jit(solution)/shard_map/while/body/eval_jaxpr/ppermute | solution.py:16
  128.0 15.4 %collective-permute-start = (bf16[256,2,1024]{2,0,1:T(8,128)(2,1)}, bf16[256,2,1024]{2,0,1:T(8,128)(2,1)}, u32[]{:S(2)}, u32[]{:S(2)}) collective-permute-start(bf16[256,2,1024]{2,0,1:T(8,128)(2,1)} %copy.84), channel_id=1, source_target_pairs={{28,0},{0,4},{4,8},{8,12},{12,16},{16,20},{20,24},{24,28},{29,1},{... | collective-permute-start | bytes 3145736 | tf_op jit(solution)/shard_map/while/body/eval_jaxpr/ppermute | solution.py:16
  145.7 15.4 %collective-permute-start = (bf16[256,2,1024]{2,0,1:T(8,128)(2,1)}, bf16[256,2,1024]{2,0,1:T(8,128)(2,1)}, u32[]{:S(2)}, u32[]{:S(2)}) collective-permute-start(bf16[256,2,1024]{2,0,1:T(8,128)(2,1)} %copy.84), channel_id=1, source_target_pairs={{28,0},{0,4},{4,8},{8,12},{12,16},{16,20},{20,24},{24,28},{29,1},{... | collective-permute-start | bytes 3145736 | tf_op jit(solution)/shard_map/while/body/eval_jaxpr/ppermute | solution.py:16
  163.4 15.4 %collective-permute-start = (bf16[256,2,1024]{2,0,1:T(8,128)(2,1)}, bf16[256,2,1024]{2,0,1:T(8,128)(2,1)}, u32[]{:S(2)}, u32[]{:S(2)}) collective-permute-start(bf16[256,2,1024]{2,0,1:T(8,128)(2,1)} %copy.84), channel_id=1, source_target_pairs={{28,0},{0,4},{4,8},{8,12},{12,16},{16,20},{20,24},{24,28},{29,1},{... | collective-permute-start | bytes 3145736 | tf_op jit(solution)/shard_map/while/body/eval_jaxpr/ppermute | solution.py:16
  181.1 15.4 %collective-permute-start = (bf16[256,2,1024]{2,0,1:T(8,128)(2,1)}, bf16[256,2,1024]{2,0,1:T(8,128)(2,1)}, u32[]{:S(2)}, u32[]{:S(2)}) collective-permute-start(bf16[256,2,1024]{2,0,1:T(8,128)(2,1)} %copy.84), channel_id=1, source_target_pairs={{28,0},{0,4},{4,8},{8,12},{12,16},{16,20},{20,24},{24,28},{29,1},{... | collective-permute-start | bytes 3145736 | tf_op jit(solution)/shard_map/while/body/eval_jaxpr/ppermute | solution.py:16
  196.5 5.1 %copy-start = (f32[8,2,1536]{2,1,0:T(2,128)}, f32[8,2,1536]{2,1,0:T(2,128)S(1)}, u32[]{:S(2)}) copy-start(f32[8,2,1536]{2,1,0:T(2,128)S(1)} %get-tuple-element.214) | copy-start | bytes 294916
